TPU v7x, 32 devices: a whole 2x2x4 slice. The times are simulated.
32 devices in a mesh: ctx: 16 (over z, y, core), head: 2 (over x).
Axes of the slice: x: 2, y: 2, z: 4, core: 2. Of those that a mesh axis runs over, the one named last changes fastest.
Arguments:
- queries: bfloat16 [16, 1024, 2048], P('ctx', None, 'head'), may hold values from -8 to 8
- keys: bfloat16 [16, 1024, 2048], P('ctx', None, 'head'), may hold values from -8 to 8
- values: bfloat16 [16, 1024, 2048], P('ctx', None, 'head'), may hold values from -24 to 24
- w_out: bfloat16 [2048, 4096], P('head'), may hold values from -0.125 to 0.125
Outputs:
- mixed: bfloat16 [16, 1024, 4096], P('ctx', 'head')
All inputs are finite; a program needn't handle non-finite values.
Results may differ from a plain program's by a relative error of at most 0.013.
Values may be sent and summed in bfloat16 or wider, within the bound.
A program may use at most 128 MiB of HBM per device.

v0:
```python
import jax
import jax.numpy as jnp
from jax import lax
from jax.sharding import PartitionSpec as P

HD = 128
GROUP = 4


masked_score = -1e30


def split_kinds(tensor, parity):
    groups = tensor.shape[2] // (2 * GROUP * HD)
    shaped = tensor.reshape((tensor.shape[0], tensor.shape[1], groups, 2, GROUP, HD))
    return shaped[:, :, :, parity].reshape((tensor.shape[0], tensor.shape[1], groups * GROUP, HD))


def normalized(scores):
    top = jnp.max(scores, axis=-1, keepdims=True)
    expo = jnp.exp(scores - top)
    total = jnp.sum(expo, axis=-1, keepdims=True)
    return (expo / total).astype(jnp.bfloat16)


def row_attention(queries, keys, values):
    scale = jnp.float32(1.0 / HD**0.5)
    length = queries.shape[1]
    causal = lax.broadcasted_iota(jnp.int32, (length, length), 1) <= lax.broadcasted_iota(
        jnp.int32, (length, length), 0
    )

    def one_row(triple):
        query_row, key_row, value_row = triple
        scores = (
            jnp.einsum("qhd,khd->hqk", query_row, key_row, preferred_element_type=jnp.float32)
            * scale
        )
        scores = jnp.where(causal, scores, masked_score)
        weights = normalized(scores)
        return jnp.einsum(
            "hqk,khd->qhd", weights, value_row, preferred_element_type=jnp.float32
        ).astype(jnp.bfloat16)

    return lax.map(one_row, (queries, keys, values))


def column_attention(triple):
    queries, keys, values = triple
    scale = jnp.float32(1.0 / HD**0.5)
    height = queries.shape[0]
    causal = lax.broadcasted_iota(jnp.int32, (height, height), 1) <= lax.broadcasted_iota(
        jnp.int32, (height, height), 0
    )
    scores = (
        jnp.einsum("rchd,schd->chrs", queries, keys, preferred_element_type=jnp.float32) * scale
    )
    scores = jnp.where(causal, scores, masked_score)
    weights = normalized(scores)
    attended = jnp.einsum(
        "chrs,schd->rchd", weights, values, preferred_element_type=jnp.float32
    ).astype(jnp.bfloat16)
    return lax.all_to_all(attended, "ctx", split_axis=0, concat_axis=1, tiled=True)


def on_device(queries, keys, values, w_out):
    rows_dev, stride, local_feat = queries.shape
    model_width = w_out.shape[1]
    groups = local_feat // (2 * GROUP * HD)
    row_out = row_attention(split_kinds(queries, 0), split_kinds(keys, 0), split_kinds(values, 0))
    col_triple = (split_kinds(queries, 1), split_kinds(keys, 1), split_kinds(values, 1))
    col_out = column_attention(
        (
            lax.all_to_all(col_triple[0], "ctx", split_axis=1, concat_axis=0, tiled=True),
            lax.all_to_all(col_triple[1], "ctx", split_axis=1, concat_axis=0, tiled=True),
            lax.all_to_all(col_triple[2], "ctx", split_axis=1, concat_axis=0, tiled=True),
        )
    )
    shaped = w_out.reshape((groups, 2, GROUP * HD, model_width))
    row_weights = shaped[:, 0].reshape((groups * GROUP * HD, model_width))
    col_weights = shaped[:, 1].reshape((groups * GROUP * HD, model_width))
    partial_value = jnp.dot(
        row_out.reshape((rows_dev * stride, -1)), row_weights, preferred_element_type=jnp.float32
    )
    partial_value = partial_value + jnp.dot(
        col_out.reshape((rows_dev * stride, -1)), col_weights, preferred_element_type=jnp.float32
    )
    partial_value = partial_value.reshape((rows_dev, stride, model_width))
    return lax.psum_scatter(
        partial_value.astype(jnp.bfloat16), "head", scatter_dimension=1, tiled=True
    )


def solution(mesh):
    return jax.shard_map(
        on_device,
        mesh=mesh,
        in_specs=(
            P("ctx", None, "head"),
            P("ctx", None, "head"),
            P("ctx", None, "head"),
            P("head", None),
        ),
        out_specs=P("ctx", "head", None),
        check_vma=False,
    )
```

profile of v0, /device:TPU:29, one launch (start us, length us, event | category | flops | bytes accessed | tf_op | source)
XLA Modules:
  0.0 252.7 jit_solution(13111694995554107261)
XLA Ops:
  6.5 2.9 %copy.35 = bf16[1,1024,1024]{1,2,0:T(8,128)(2,1)S(1)} copy(bf16[1,1024,1024]{2,1,0:T(8,128)(2,1)} %param.4) | data formatting | bytes 4194304 | tf_op args[0]
  9.4 0.0 copy-start
  9.4 0.1 slice_bitcast_fusion.6
  9.5 1.6 copy.41
  11.1 6.3 %all-to-all-start = ((bf16[1,1024,4,128]{3,2,0,1:T(4,128)(2,1)}), bf16[1,1024,4,128]{3,2,0,1:T(4,128)(2,1)S(1)}, u32[]{:S(2)}, u32[]{:S(2)}) async-start(bf16[1,1024,4,128]{3,2,0,1:T(4,128)(2,1)} %copy.41), calls=%async_computation | async-start | bytes 2097152 | tf_op jit(solution)/shard_map/all_to_all | solution.py:74
  17.4 4.0 %copy.37 = bf16[1,1024,1024]{1,2,0:T(8,128)(2,1)} copy(bf16[1,1024,1024]{2,1,0:T(8,128)(2,1)} %param.5) | data formatting | bytes 4194304 | tf_op args[1]
  21.3 0.0 copy-done
  21.4 1.3 slice_bitcast_fusion.5
  22.6 1.4 copy.43
  24.1 17.3 %all-to-all-done = bf16[1,1024,4,128]{3,2,0,1:T(4,128)(2,1)S(1)} async-done(((bf16[1,1024,4,128]{3,2,0,1:T(4,128)(2,1)}), bf16[1,1024,4,128]{3,2,0,1:T(4,128)(2,1)S(1)}, u32[]{:S(2)}, u32[]{:S(2)}) %all-to-all-start) | async-done | bytes 1048608 | tf_op jit(solution)/shard_map/all_to_all | solution.py:74
  41.3 0.0 copy-start.1
  41.3 5.7 %all-to-all-start.1 = ((bf16[1,1024,4,128]{3,2,0,1:T(4,128)(2,1)}), bf16[1,1024,4,128]{3,2,0,1:T(4,128)(2,1)}, u32[]{:S(2)}, u32[]{:S(2)}) async-start(bf16[1,1024,4,128]{3,2,0,1:T(4,128)(2,1)} %copy.43), calls=%async_computation.1 | async-start | bytes 2097152 | tf_op jit(solution)/shard_map/all_to_all | solution.py:75
  47.1 2.9 %copy.39 = bf16[1,1024,1024]{1,2,0:T(8,128)(2,1)S(1)} copy(bf16[1,1024,1024]{2,1,0:T(8,128)(2,1)} %param.6) | data formatting | bytes 4194304 | tf_op args[2]
  49.9 0.0 copy-done.1
  50.0 0.1 slice_bitcast_fusion.4
  50.0 1.5 copy.47
  51.5 19.6 %all-to-all-done.1 = bf16[1,1024,4,128]{3,2,0,1:T(4,128)(2,1)} async-done(((bf16[1,1024,4,128]{3,2,0,1:T(4,128)(2,1)}), bf16[1,1024,4,128]{3,2,0,1:T(4,128)(2,1)}, u32[]{:S(2)}, u32[]{:S(2)}) %all-to-all-start.1) | async-done | bytes 1048608 | tf_op jit(solution)/shard_map/all_to_all | solution.py:75
  71.1 5.7 %all-to-all-start.2 = ((bf16[1,1024,4,128]{3,2,0,1:T(4,128)(2,1)}), bf16[1,1024,4,128]{3,2,0,1:T(4,128)(2,1)}, u32[]{:S(2)}, u32[]{:S(2)}) async-start(bf16[1,1024,4,128]{3,2,0,1:T(4,128)(2,1)} %copy.47), calls=%async_computation.2 | async-start | bytes 2097152 | tf_op jit(solution)/shard_map/all_to_all | solution.py:76
  76.9 1.3 iota_compare_fusion
  78.2 0.0 copy-start.2
  78.2 11.8 %fusion.29 = (f32[4,1024]{1,0:T(4,128)S(1)}, f32[4,1024,1024]{1,2,0:T(8,128)}) fusion(pred[1024,1024]{0,1:T(8,128)(4,1)} %iota_compare_fusion, bf16[1,1024,1,2,4,128]{1,5,4,3,2,0:T(8,128)(2,1)} %bitcast.62, bf16[1,1024,1,2,4,128]{1,5,4,3,2,0:T(8,128)(2,1)} %bitcast.64), kind=kOutput, calls=%fused_computation.46 | convolution fusion | flops 1090520064 | bytes 19939328 | tf_op jit(solution)/shard_map/while/body/eval_jaxpr/sub | solution.py:21
  90.0 0.0 copy-done.2
  90.0 4.6 %fusion.30 = (f32[64,4,16]{2,1,0:T(4,128)S(1)}, f32[64,4,16,16]{2,3,1,0:T(8,128)}) fusion(pred[16,16]{0,1:T(8,128)(4,1)S(1)} %iota_compare_fusion.1, bf16[16,64,4,128]{3,2,1,0:T(4,128)(2,1)} %bitcast.13, bf16[16,64,4,128]{3,2,1,0:T(4,128)(2,1)S(1)} %bitcast.65), kind=kOutput, calls=%fused_computation.47 | convolution fusion | flops 17039376 | bytes 2375936 | tf_op jit(solution)/shard_map/sub | solution.py:21
  94.6 6.3 %all-to-all-done.2 = bf16[1,1024,4,128]{3,2,0,1:T(4,128)(2,1)} async-done(((bf16[1,1024,4,128]{3,2,0,1:T(4,128)(2,1)}), bf16[1,1024,4,128]{3,2,0,1:T(4,128)(2,1)}, u32[]{:S(2)}, u32[]{:S(2)}) %all-to-all-start.2) | async-done | bytes 1048608 | tf_op jit(solution)/shard_map/all_to_all | solution.py:76
  100.9 2.7 %fusion.13 = bf16[16,64,4,128]{3,0,2,1:T(8,128)(2,1)S(1)} fusion(f32[64,4,16,16]{2,3,1,0:T(8,128)} %get-tuple-element.24, bf16[16,64,4,128]{3,2,1,0:T(4,128)(2,1)} %bitcast.15, f32[64,4,16]{2,1,0:T(4,128)S(1)} %get-tuple-element.17), kind=kOutput, calls=%fused_computation.23 | convolution fusion | flops 17432576 | bytes 2375680 | tf_op jit(solution)/shard_map/chrs,schd->rchd/dot_general | solution.py:60
  103.7 1.5 copy.51
  105.1 5.7 %all-to-all-start.3 = ((bf16[16,64,4,128]{3,2,1,0:T(4,128)(2,1)}), bf16[16,64,4,128]{3,2,1,0:T(4,128)(2,1)S(1)}, u32[]{:S(2)}, u32[]{:S(2)}) async-start(bf16[16,64,4,128]{3,2,1,0:T(4,128)(2,1)} %copy.51), calls=%async_computation.3 | async-start | bytes 2097152 | tf_op jit(solution)/shard_map/all_to_all | solution.py:63
  110.9 0.2 reduce-scatter.2.cloned.1.call-start
  111.1 7.1 %fusion.12 = bf16[4,1024,128]{1,2,0:T(8,128)(2,1)S(1)} fusion(f32[4,1024,1024]{1,2,0:T(8,128)} %get-tuple-element.16, f32[4,1024]{1,0:T(4,128)S(1)} %get-tuple-element.15, bf16[1,1024,1,2,4,128]{1,5,4,3,2,0:T(8,128)(2,1)S(1)} %bitcast.60), kind=kOutput, calls=%fused_computation.21 | convolution fusion | flops 1082654720 | bytes 18890752 | tf_op jit(solution)/shard_map/while/body/eval_jaxpr/hqk,khd->qhd/dot_general | solution.py:41
  118.2 10.3 %fusion.8 = f32[1024,4096]{1,0:T(8,128)} fusion(bf16[1024,512]{0,1:T(8,128)(2,1)S(1)} %bitcast.69, bf16[1,2,512,4096]{3,2,1,0:T(8,128)(2,1)} %bitcast.67), kind=kOutput, calls=%fused_computation.14 | convolution fusion | flops 4294967296 | bytes 22020096 | tf_op jit(solution)/shard_map/dot_general | solution.py:82
  128.5 6.3 %all-to-all-done.3 = bf16[16,64,4,128]{3,2,1,0:T(4,128)(2,1)S(1)} async-done(((bf16[16,64,4,128]{3,2,1,0:T(4,128)(2,1)}), bf16[16,64,4,128]{3,2,1,0:T(4,128)(2,1)S(1)}, u32[]{:S(2)}, u32[]{:S(2)}) %all-to-all-start.3) | async-done | bytes 1048608 | tf_op jit(solution)/shard_map/all_to_all | solution.py:63
  134.8 11.3 %fusion.3 = bf16[1,1024,4096]{2,1,0:T(8,128)(2,1)} fusion(f32[1024,4096]{1,0:T(8,128)} %fusion.8, bf16[1,2,512,4096]{3,2,1,0:T(8,128)(2,1)} %bitcast.68, bf16[128,8,4,128]{3,2,1,0:T(4,128)(2,1)S(1)} %bitcast.66), kind=kOutput, calls=%fused_computation.7 | convolution fusion | flops 4303355904 | bytes 30408704 | tf_op jit(solution)/shard_map/dot_general | solution.py:85
  146.1 0.0 reduce-scatter.2.cloned.1.call-update
  146.1 99.7 %reduce-scatter.2.cloned.1.call-done = bf16[1,512,4096]{2,1,0:T(8,128)(2,1)} async-done(((bf16[1,1024,4096]{2,1,0:T(8,128)(2,1)}), bf16[1,512,4096]{2,1,0:T(8,128)(2,1)}) %reduce-scatter.2.cloned.1.call-update) | async-done | bytes 4194320 | tf_op jit(solution)/shard_map/reduce_scatter | solution.py:89
  (1 shorter events, 0.0 us)
Async XLA Ops:
  9.4 12.0 %copy-start = (bf16[1,1024,1024]{1,2,0:T(8,128)(2,1)}, bf16[1,1024,1024]{1,2,0:T(8,128)(2,1)S(1)}, u32[]{:S(2)}) copy-start(bf16[1,1024,1024]{1,2,0:T(8,128)(2,1)S(1)} %copy.35) | copy-start | bytes 6291460
  11.1 30.2 %all-to-all-start = ((bf16[1,1024,4,128]{3,2,0,1:T(4,128)(2,1)}), bf16[1,1024,4,128]{3,2,0,1:T(4,128)(2,1)S(1)}, u32[]{:S(2)}, u32[]{:S(2)}) async-start(bf16[1,1024,4,128]{3,2,0,1:T(4,128)(2,1)} %copy.41), calls=%async_computation | async-start | bytes 2097152 | tf_op jit(solution)/shard_map/all_to_all | solution.py:74
  41.3 8.6 %copy-start.1 = (bf16[1,1024,4,128]{3,2,0,1:T(4,128)(2,1)}, bf16[1,1024,4,128]{3,2,0,1:T(4,128)(2,1)S(1)}, u32[]{:S(2)}) copy-start(bf16[1,1024,4,128]{3,2,0,1:T(4,128)(2,1)S(1)} %all-to-all-done) | copy-start | bytes 3145732
  41.3 29.8 %all-to-all-start.1 = ((bf16[1,1024,4,128]{3,2,0,1:T(4,128)(2,1)}), bf16[1,1024,4,128]{3,2,0,1:T(4,128)(2,1)}, u32[]{:S(2)}, u32[]{:S(2)}) async-start(bf16[1,1024,4,128]{3,2,0,1:T(4,128)(2,1)} %copy.43), calls=%async_computation.1 | async-start | bytes 2097152 | tf_op jit(solution)/shard_map/all_to_all | solution.py:75
  71.1 29.8 %all-to-all-start.2 = ((bf16[1,1024,4,128]{3,2,0,1:T(4,128)(2,1)}), bf16[1,1024,4,128]{3,2,0,1:T(4,128)(2,1)}, u32[]{:S(2)}, u32[]{:S(2)}) async-start(bf16[1,1024,4,128]{3,2,0,1:T(4,128)(2,1)} %copy.47), calls=%async_computation.2 | async-start | bytes 2097152 | tf_op jit(solution)/shard_map/all_to_all | solution.py:76
  78.2 11.8 %copy-start.2 = (bf16[1,1024,4,128]{3,2,0,1:T(4,128)(2,1)S(1)}, bf16[1,1024,4,128]{3,2,0,1:T(4,128)(2,1)}, u32[]{:S(2)}) copy-start(bf16[1,1024,4,128]{3,2,0,1:T(4,128)(2,1)} %copy-done.1) | copy-start | bytes 3145732
  105.1 29.7 %all-to-all-start.3 = ((bf16[16,64,4,128]{3,2,1,0:T(4,128)(2,1)}), bf16[16,64,4,128]{3,2,1,0:T(4,128)(2,1)S(1)}, u32[]{:S(2)}, u32[]{:S(2)}) async-start(bf16[16,64,4,128]{3,2,1,0:T(4,128)(2,1)} %copy.51), calls=%async_computation.3 | async-start | bytes 2097152 | tf_op jit(solution)/shard_map/all_to_all | solution.py:63
  110.9 135.0 %reduce-scatter.2.cloned.1.call-start = ((), (), s32[]{:S(2)}) async-start(), calls=%async_computation.5 | async-start | bytes 12582912 | tf_op jit(solution)/shard_map/reduce_scatter | solution.py:89
Sparse Core Ops, SparseCore 0:
  146.2 99.5 reduce-scatter.1
where the time goes:
time: 255 us; the launch traced here: 253 us
  waiting for transfers between devices  149 us (58%)
  matrix products  47.8 us (19%)
  starting transfers between devices  23.7 us (9%)
  local copies, waits for them, and re-layouts  17.1 us (7%)
  between operations  13.5 us (5%)
    reduce_scatter x1, waiting for transfers between devices, on_device(): lax.psum_scatter(partial_value.astype(jnp.bfloat16), 'head', scatter_dime...  99.7 us
    all_to_all x1, waiting for transfers between devices, on_device(): lax.all_to_all(col_triple[1], 'ctx', split_axis=1, concat_axis=0, tiled=T...  19.6 us
    all_to_all x1, waiting for transfers between devices, on_device(): lax.all_to_all(col_triple[0], 'ctx', split_axis=1, concat_axis=0, tiled=T...  17.3 us
    sub x2, matrix products, normalized(): expo = jnp.exp(scores - top)  16.4 us
    dot_general x1, matrix products, on_device(): jnp.dot(col_out.reshape((rows_dev * stride, -1)), col_weights, preferred_...  11.3 us
    dot_general x1, matrix products, on_device(): jnp.dot(row_out.reshape((rows_dev * stride, -1)), row_weights, preferred_...  10.3 us
    unnamed x9, local copies, waits for them, and re-layouts  9.68 us
    dot_general x1, matrix products, one_row(): jnp.einsum('hqk,khd->qhd', weights, value_row, preferred_element_type=jnp...  7.07 us
  transfers between devices with their start and end apart: 5, of which 5 were waited for; matrix products, arithmetic and copies ran while one was open for 18% of the time, Pallas kernels for 0%

commit v1 on v0

v1 whole, which is shorter than its diff:
```python
import functools

import jax
import jax.numpy as jnp
from jax import lax
from jax.experimental import pallas as pl
from jax.experimental.pallas import tpu as pltpu
from jax.sharding import PartitionSpec as P

HD = 128
GROUP = 4
MESH = pl.DeviceIdType.MESH
PIECES = 4

masked_score = -1e30


def attend(query, key, value, allowed):
    scores = lax.dot_general(
        query, key, (((1,), (1,)), ((), ())), preferred_element_type=jnp.float32
    ) * jnp.float32(1.0 / HD**0.5)
    scores = jnp.where(allowed, scores, masked_score)
    top = jnp.max(scores, axis=-1, keepdims=True)
    expo = jnp.exp(scores - top)
    total = jnp.sum(expo, axis=-1, keepdims=True)
    mixed = jnp.dot(expo.astype(jnp.bfloat16), value, preferred_element_type=jnp.float32)
    return (mixed / total).astype(jnp.bfloat16)


def body(
    n, q_hbm, k_hbm, v_hbm, w_hbm, out_ref, q_row, k_row, v_row, q_col, k_col, v_col,
    col_out, row_out, joined, w_own, w_other, local_sem, in_send, in_recv, back_send, back_recv,
    w_send, w_recv, row_send, row_recv,
):
    me, head = lax.axis_index("ctx"), lax.axis_index("head")
    other = 1 - head
    stride = q_hbm.shape[1]
    block = q_row.shape[1]
    depth = w_own.shape[0]
    half = joined.shape[1]
    cols = stride // n
    hbm = (q_hbm, k_hbm, v_hbm)
    rows_in = (q_row, k_row, v_row)
    cols_in = (q_col, k_col, v_col)
    back_head = lax.div(me * cols, half)
    member = lax.rem(me, 4)
    sibling = me + 1 - 2 * lax.rem(me, 2)
    beside = me + 2 - 4 * lax.div(member, 2)
    piece = depth // (4 * PIECES)

    def col_copy(t, d):
        peer = lax.rem(me + d, n)
        return pltpu.make_async_remote_copy(
            src_ref=hbm[t].at[0, pl.ds(peer * cols, cols), pl.ds(block, block)],
            dst_ref=cols_in[t].at[me],
            send_sem=in_send.at[t, d],
            recv_sem=in_recv.at[t, d],
            device_id=(peer, head),
            device_id_type=MESH,
        )

    def col_arrival(t, d):
        source = lax.rem(me + n - d, n)
        return pltpu.make_async_remote_copy(
            src_ref=hbm[t].at[0, pl.ds(0, cols), pl.ds(block, block)],
            dst_ref=cols_in[t].at[source],
            send_sem=in_send.at[t, d],
            recv_sem=in_recv.at[t, d],
            device_id=(source, head),
            device_id_type=MESH,
        )

    def w_copy(source, index, way, to_ctx, to_head):
        rows = pl.ds(index * piece, piece)
        return pltpu.make_async_remote_copy(
            src_ref=source.at[rows],
            dst_ref=w_other.at[rows],
            send_sem=w_send.at[way, index],
            recv_sem=w_recv.at[index],
            device_id=(to_ctx, to_head),
            device_id_type=MESH,
        )

    def index_of(who, s):
        return who * PIECES + s

    member_sibling = lax.rem(sibling, 4)
    member_beside = lax.rem(beside, 4)
    member_far = lax.rem(member + 2, 4) + 1 - 2 * lax.rem(member, 2)

    for t in range(3):

        @pl.loop(1, n)
        def _(d):
            col_copy(t, d).start()

    @pl.loop(0, PIECES)
    def _(s):
        w_copy(w_hbm, index_of(member, s), 0, me, other).start()

    local = [
        pltpu.make_async_copy(hbm[t].at[0, :, pl.ds(0, block)], rows_in[t], local_sem.at[t])
        for t in range(3)
    ]
    local += [
        pltpu.make_async_copy(
            hbm[t].at[0, pl.ds(me * cols, cols), pl.ds(block, block)],
            cols_in[t].at[me],
            local_sem.at[3 + t],
        )
        for t in range(3)
    ]
    local.append(pltpu.make_async_copy(w_hbm, w_own, local_sem.at[6]))
    for copy in local:
        copy.start()
    for copy in local[:3]:
        copy.wait()

    tile = min(256, half)
    row_index = lax.broadcasted_iota(jnp.int32, (tile, stride), 0)
    key_index = lax.broadcasted_iota(jnp.int32, (tile, stride), 1)

    @pl.loop(0, block // HD)
    def _(h):
        lanes = pl.ds(pl.multiple_of(h * HD, HD), HD)
        for start in range(0, stride, tile):
            end = start + tile
            row_out[pl.ds(start, tile), lanes] = attend(
                q_row[pl.ds(start, tile), lanes],
                k_row[pl.ds(0, end), lanes],
                v_row[pl.ds(0, end), lanes],
                key_index[:, :end] <= row_index[:, :end] + start,
            )

    row_copy = pltpu.make_async_remote_copy(
        src_ref=row_out.at[pl.ds(pl.multiple_of(other * half, half), half)],
        dst_ref=joined.at[head, :, pl.ds(0, block)],
        send_sem=row_send,
        recv_sem=row_recv,
        device_id=(me, other),
        device_id_type=MESH,
    )
    row_copy.start()
    joined[head, :, pl.ds(0, block)] = row_out[pl.ds(pl.multiple_of(head * half, half), half)]

    @pl.loop(0, PIECES)
    def _(s):
        index = index_of(member, s)
        w_copy(w_hbm, index, 0, me, other).wait_recv()
        w_copy(w_other, index, 1, beside, head).start()
        w_copy(w_other, index, 2, sibling, head).start()

    for copy in local[3:]:
        copy.wait()
    for t in range(3):

        @pl.loop(1, n)
        def _(d):
            col_arrival(t, d).wait_recv()

    width = min(cols, max(16, 256 // n))
    size = n * width
    r_index = lax.broadcasted_iota(jnp.int32, (size, size), 0)
    s_index = lax.broadcasted_iota(jnp.int32, (size, size), 1)
    allowed = (s_index <= r_index) & (((r_index - s_index) & (width - 1)) == 0)

    @pl.loop(0, block // HD)
    def _(h):
        lanes = pl.ds(pl.multiple_of(h * HD, HD), HD)
        for start in range(0, cols, width):
            at = (slice(None), pl.ds(start, width), lanes)
            got = attend(*(ref[at].reshape(size, HD) for ref in cols_in), allowed)
            col_out[at] = got.reshape(n, width, HD)

    def back_copy(r):
        slot = lax.rem(me, n // 2)
        return pltpu.make_async_remote_copy(
            src_ref=col_out.at[r],
            dst_ref=joined.at[head, pl.ds(pl.multiple_of(slot * cols, cols), cols), pl.ds(block, block)],
            send_sem=back_send.at[r],
            recv_sem=back_recv.at[head, slot],
            device_id=(r, back_head),
            device_id_type=MESH,
        )

    def back_arrival(source_head, slot):
        return pltpu.make_async_remote_copy(
            src_ref=col_out.at[0],
            dst_ref=joined.at[
                source_head, pl.ds(pl.multiple_of(slot * cols, cols), cols), pl.ds(block, block)
            ],
            send_sem=back_send.at[0],
            recv_sem=back_recv.at[source_head, slot],
            device_id=(me, other),
            device_id_type=MESH,
        )

    stays = back_head == head

    @pl.loop(1, n)
    def _(d):
        back_copy(lax.rem(me + d, n)).start()

    @pl.when(stays)
    def _():
        slot = lax.rem(me, n // 2)
        joined[head, pl.ds(pl.multiple_of(slot * cols, cols), cols), pl.ds(block, block)] = col_out[me]

    @pl.when(jnp.logical_not(stays))
    def _():
        back_copy(me).start()

    @pl.loop(0, PIECES)
    def _(s):
        index = index_of(member_beside, s)
        w_copy(w_other, index, 1, beside, head).wait_recv()
        w_copy(w_other, index, 3, sibling, head).start()

    row_copy.wait_recv()

    @pl.loop(0, PIECES)
    def _(s):
        w_copy(w_other, index_of(member_sibling, s), 2, sibling, head).wait_recv()
        w_copy(w_other, index_of(member_far, s), 3, sibling, head).wait_recv()

    for source_head in range(2):

        @pl.loop(0, n // 2)
        def _(slot):
            mine = (head * (n // 2) + slot == me) & (head == source_head)

            @pl.when(jnp.logical_not(mine))
            def _():
                back_arrival(source_head, slot).wait_recv()

    step = 512

    @pl.loop(0, out_ref.shape[1] // step)
    def _(c):
        lanes = pl.ds(pl.multiple_of(c * step, step), step)
        total = jnp.dot(joined[head], w_own[:, lanes], preferred_element_type=jnp.float32)
        total += jnp.dot(joined[other], w_other[:, lanes], preferred_element_type=jnp.float32)
        out_ref[:, lanes] = total.astype(jnp.bfloat16)

    for t in range(3):

        @pl.loop(1, n)
        def _(d):
            col_copy(t, d).wait_send()

    @pl.loop(0, PIECES)
    def _(s):
        w_copy(w_hbm, index_of(member, s), 0, me, other).wait_send()
        w_copy(w_other, index_of(member, s), 1, beside, head).wait_send()
        w_copy(w_other, index_of(member, s), 2, sibling, head).wait_send()
        w_copy(w_other, index_of(member_beside, s), 3, sibling, head).wait_send()

    row_copy.wait_send()

    @pl.loop(1, n)
    def _(d):
        back_copy(lax.rem(me + d, n)).wait_send()

    @pl.when(jnp.logical_not(stays))
    def _():
        back_copy(me).wait_send()


def on_device(n, queries, keys, values, w_out):
    _, stride, local_feat = queries.shape
    depth, model_width = w_out.shape
    block = GROUP * HD
    assert queries.shape[0] == 1 and local_feat == 2 * block
    half = stride // lax.axis_size("head")
    cols = stride // n
    bf16 = jnp.bfloat16
    dma = pltpu.SemaphoreType.DMA
    out = pl.pallas_call(
        functools.partial(body, n),
        out_shape=jax.ShapeDtypeStruct((half, model_width), bf16),
        in_specs=[pl.BlockSpec(memory_space=pltpu.HBM)] * 4,
        out_specs=pl.BlockSpec(memory_space=pltpu.VMEM),
        scratch_shapes=[pltpu.VMEM((stride, block), bf16)] * 3
        + [pltpu.VMEM((n, cols, block), bf16)] * 4
        + [
            pltpu.VMEM((stride, block), bf16),
            pltpu.VMEM((2, half, local_feat), bf16),
            pltpu.VMEM((depth, model_width), bf16),
            pltpu.VMEM((depth, model_width), bf16),
            dma((7,)),
            dma((3, n)),
            dma((3, n)),
            dma((n,)),
            dma((2, n // 2)),
            dma((4, 4 * PIECES)),
            dma((4 * PIECES,)),
            dma,
            dma,
        ],
        compiler_params=pltpu.CompilerParams(has_side_effects=True, vmem_limit_bytes=60 * 2**20),
    )(queries, keys, values, w_out)
    return out.reshape((1, half, model_width))


def solution(mesh):
    return jax.shard_map(
        functools.partial(on_device, mesh.shape["ctx"]),
        mesh=mesh,
        in_specs=(
            P("ctx", None, "head"),
            P("ctx", None, "head"),
            P("ctx", None, "head"),
            P("head", None),
        ),
        out_specs=P("ctx", "head", None),
        check_vma=False,
    )
```

time: 255 us -> 127 us (0.50)
  waiting for transfers between devices: 149 us -> 0 us
  Pallas kernels: 0 us -> 122 us
  matrix products: 47.8 us -> 0 us
  starting transfers between devices: 23.7 us -> 0 us
  between operations: 13.5 us -> 0.01 us
  local copies, waits for them, and re-layouts: 17.1 us -> 4.7 us
    pallas_call x0 -> x1, Pallas kernels: none -> 122 us  [on_device(): pl.pallas_call(functools.partial(body, n), out_shape=jax.ShapeDtypeStruct...]
    reduce_scatter x1 -> x0, waiting for transfers between devices: 99.7 us -> none  [on_device(): lax.psum_scatter(partial_value.astype(jnp.bfloat16), 'head', scatter_dime...]
    all_to_all x4 -> x0, waiting for transfers between devices: 49.6 us -> none  [the longest x1 19.6 us: on_device(): lax.all_to_all(col_triple[1], 'ctx', split_axis=1, concat_axis=0, tiled=T...]
    dot_general x4 -> x0, matrix products: 31.4 us -> none  [the longest x1 11.3 us: on_device(): jnp.dot(col_out.reshape((rows_dev * stride, -1)), col_weights, preferred_...]
    all_to_all x4 -> x0, starting transfers between devices: 23.5 us -> none  [the longest x1 6.3 us: on_device(): lax.all_to_all(col_triple[0], 'ctx', split_axis=1, concat_axis=0, tiled=T...]
    sub x2 -> x0, matrix products: 16.4 us -> none  [normalized(): expo = jnp.exp(scores - top)]
    another operation x6 -> x0, local copies, waits for them, and re-layouts: 5.93 us -> none  [split_kinds(): shaped[:, :, :, parity]]
    unnamed x9 -> x1, local copies, waits for them, and re-layouts: 9.68 us -> 4.7 us
  transfers between devices with their start and end apart: 5 -> 0, of which waited for: 5 -> 0; matrix products, arithmetic and copies ran while one was open for 18% -> 0% of each run, Pallas kernels for 0% -> 0%
where the time goes in v1:
time: 127 us
  Pallas kernels  122 us (96%)
  local copies, waits for them, and re-layouts  4.7 us (4%)
    pallas_call x1, Pallas kernels, on_device(): pl.pallas_call(functools.partial(body, n), out_shape=jax.ShapeDtypeStruct...  122 us
    unnamed x1, local copies, waits for them, and re-layouts  4.7 us

profile of v1, /device:TPU:29, one launch (start us, length us, event | category | flops | bytes accessed | tf_op | source)
XLA Modules:
  0.0 127.1 jit_solution(11756203983779841808)
XLA Ops:
  0.0 122.4 %shard_map.46 = bf16[512,4096]{1,0:T(8,128)(2,1)} custom-call(bf16[1,1024,1024]{2,1,0:T(8,128)(2,1)} %q_hbm.1, bf16[1,1024,1024]{2,1,0:T(8,128)(2,1)} %k_hbm.1, bf16[1,1024,1024]{2,1,0:T(8,128)(2,1)} %v_hbm.1, bf16[1024,4096]{1,0:T(8,128)(2,1)} %w_hbm.1), custom_call_target="tpu_custom_call" | custom-call | tf_op jit(solution)/shard_map/pallas_call | solution.py:278
  122.4 4.7 %copy.6 = bf16[1,512,4096]{2,1,0:T(8,128)(2,1)} copy(bf16[1,512,4096]{2,1,0:T(8,128)(2,1)} %bitcast.1) | data formatting | bytes 8388608

commit v2 on v1

--- a/solution.py
+++ b/solution.py
@@ -10,7 +10,9 @@
 HD = 128
 GROUP = 4
 MESH = pl.DeviceIdType.MESH
-PIECES = 4
+PIECES = 8
+STRAIGHT = 2
+PARTS = 2
 
 masked_score = -1e30
 
@@ -29,7 +31,7 @@
 
 def body(
     n, q_hbm, k_hbm, v_hbm, w_hbm, out_ref, q_row, k_row, v_row, q_col, k_col, v_col,
-    col_out, row_out, joined, w_own, w_other, local_sem, in_send, in_recv, back_send, back_recv,
+    col_out, row_out, joined, summed, w_own, w_other, local_sem, in_send, in_recv, back_send, back_recv,
     w_send, w_recv, row_send, row_recv,
 ):
     me, head = lax.axis_index("ctx"), lax.axis_index("head")
@@ -39,6 +41,7 @@
     depth = w_own.shape[0]
     half = joined.shape[1]
     cols = stride // n
+    share = block // PARTS
     hbm = (q_hbm, k_hbm, v_hbm)
     rows_in = (q_row, k_row, v_row)
     cols_in = (q_col, k_col, v_col)
@@ -48,24 +51,26 @@
     beside = me + 2 - 4 * lax.div(member, 2)
     piece = depth // (4 * PIECES)
 
-    def col_copy(t, d):
+    def col_copy(t, part, d):
         peer = lax.rem(me + d, n)
-        return pltpu.make_async_remote_copy(
-            src_ref=hbm[t].at[0, pl.ds(peer * cols, cols), pl.ds(block, block)],
-            dst_ref=cols_in[t].at[me],
-            send_sem=in_send.at[t, d],
-            recv_sem=in_recv.at[t, d],
+        lanes = pl.ds(part * share, share)
+        return pltpu.make_async_remote_copy(
+            src_ref=hbm[t].at[0, pl.ds(peer * cols, cols), pl.ds(block + part * share, share)],
+            dst_ref=cols_in[t].at[me, :, lanes],
+            send_sem=in_send.at[t * PARTS + part, d],
+            recv_sem=in_recv.at[t * PARTS + part, d],
             device_id=(peer, head),
             device_id_type=MESH,
         )
 
-    def col_arrival(t, d):
+    def col_arrival(t, part, d):
         source = lax.rem(me + n - d, n)
-        return pltpu.make_async_remote_copy(
-            src_ref=hbm[t].at[0, pl.ds(0, cols), pl.ds(block, block)],
-            dst_ref=cols_in[t].at[source],
-            send_sem=in_send.at[t, d],
-            recv_sem=in_recv.at[t, d],
+        lanes = pl.ds(part * share, share)
+        return pltpu.make_async_remote_copy(
+            src_ref=hbm[t].at[0, pl.ds(0, cols), pl.ds(block + part * share, share)],
+            dst_ref=cols_in[t].at[source, :, lanes],
+            send_sem=in_send.at[t * PARTS + part, d],
+            recv_sem=in_recv.at[t * PARTS + part, d],
             device_id=(source, head),
             device_id_type=MESH,
         )
@@ -88,15 +93,20 @@
     member_beside = lax.rem(beside, 4)
     member_far = lax.rem(member + 2, 4) + 1 - 2 * lax.rem(member, 2)
 
-    for t in range(3):
-
-        @pl.loop(1, n)
-        def _(d):
-            col_copy(t, d).start()
+    for part in range(PARTS):
+
+        @pl.loop(1, n)
+        def _(d):
+            for t in range(3):
+                col_copy(t, part, d).start()
 
     @pl.loop(0, PIECES)
     def _(s):
         w_copy(w_hbm, index_of(member, s), 0, me, other).start()
+
+    @pl.loop(PIECES - STRAIGHT, PIECES)
+    def _(s):
+        w_copy(w_hbm, index_of(member_beside, s), 0, me, other).start()
 
     local = [
         pltpu.make_async_copy(hbm[t].at[0, :, pl.ds(0, block)], rows_in[t], local_sem.at[t])
@@ -143,72 +153,106 @@
     row_copy.start()
     joined[head, :, pl.ds(0, block)] = row_out[pl.ds(pl.multiple_of(head * half, half), half)]
 
-    @pl.loop(0, PIECES)
-    def _(s):
-        index = index_of(member, s)
-        w_copy(w_hbm, index, 0, me, other).wait_recv()
-        w_copy(w_other, index, 1, beside, head).start()
-        w_copy(w_other, index, 2, sibling, head).start()
+    def onward(first, last):
+        @pl.loop(first, last)
+        def _(s):
+            index = index_of(member, s)
+            w_copy(w_hbm, index, 0, me, other).wait_recv()
+
+            @pl.when(s < PIECES - STRAIGHT)
+            def _():
+                w_copy(w_other, index, 1, beside, head).start()
+
+            w_copy(w_other, index, 2, sibling, head).start()
+
+    onward(0, PIECES // 2)
 
     for copy in local[3:]:
         copy.wait()
-    for t in range(3):
-
-        @pl.loop(1, n)
-        def _(d):
-            col_arrival(t, d).wait_recv()
-
+
+    step = 512
+
+    def tiles(add):
+        @pl.loop(0, out_ref.shape[1] // step)
+        def _(c):
+            add(pl.ds(pl.multiple_of(c * step, step), step))
+
+    def own_row_part(lanes):
+        summed[:, lanes] = jnp.dot(
+            joined[head, :, pl.ds(0, block)],
+            w_own[pl.ds(0, block), lanes],
+            preferred_element_type=jnp.float32,
+        )
+
+    tiles(own_row_part)
     width = min(cols, max(16, 256 // n))
     size = n * width
     r_index = lax.broadcasted_iota(jnp.int32, (size, size), 0)
     s_index = lax.broadcasted_iota(jnp.int32, (size, size), 1)
     allowed = (s_index <= r_index) & (((r_index - s_index) & (width - 1)) == 0)
 
-    @pl.loop(0, block // HD)
-    def _(h):
-        lanes = pl.ds(pl.multiple_of(h * HD, HD), HD)
-        for start in range(0, cols, width):
-            at = (slice(None), pl.ds(start, width), lanes)
-            got = attend(*(ref[at].reshape(size, HD) for ref in cols_in), allowed)
-            col_out[at] = got.reshape(n, width, HD)
-
-    def back_copy(r):
-        slot = lax.rem(me, n // 2)
-        return pltpu.make_async_remote_copy(
-            src_ref=col_out.at[r],
-            dst_ref=joined.at[head, pl.ds(pl.multiple_of(slot * cols, cols), cols), pl.ds(block, block)],
-            send_sem=back_send.at[r],
-            recv_sem=back_recv.at[head, slot],
+    slot_here = lax.rem(me, n // 2)
+    stays = back_head == head
+
+    def landing(source_head, part, slot):
+        return joined.at[
+            source_head,
+            pl.ds(pl.multiple_of(slot * cols, cols), cols),
+            pl.ds(block + part * share, share),
+        ]
+
+    def back_copy(part, r):
+        return pltpu.make_async_remote_copy(
+            src_ref=col_out.at[r, :, pl.ds(part * share, share)],
+            dst_ref=landing(head, part, slot_here),
+            send_sem=back_send.at[part, r],
+            recv_sem=back_recv.at[head * PARTS + part, slot_here],
             device_id=(r, back_head),
             device_id_type=MESH,
         )
 
-    def back_arrival(source_head, slot):
-        return pltpu.make_async_remote_copy(
-            src_ref=col_out.at[0],
-            dst_ref=joined.at[
-                source_head, pl.ds(pl.multiple_of(slot * cols, cols), cols), pl.ds(block, block)
-            ],
-            send_sem=back_send.at[0],
-            recv_sem=back_recv.at[source_head, slot],
+    def back_arrival(source_head, part, slot):
+        return pltpu.make_async_remote_copy(
+            src_ref=col_out.at[0, :, pl.ds(part * share, share)],
+            dst_ref=landing(source_head, part, slot),
+            send_sem=back_send.at[part, 0],
+            recv_sem=back_recv.at[source_head * PARTS + part, slot],
             device_id=(me, other),
             device_id_type=MESH,
         )
 
-    stays = back_head == head
-
-    @pl.loop(1, n)
-    def _(d):
-        back_copy(lax.rem(me + d, n)).start()
-
-    @pl.when(stays)
-    def _():
-        slot = lax.rem(me, n // 2)
-        joined[head, pl.ds(pl.multiple_of(slot * cols, cols), cols), pl.ds(block, block)] = col_out[me]
-
-    @pl.when(jnp.logical_not(stays))
-    def _():
-        back_copy(me).start()
+    for part in range(PARTS):
+
+        @pl.loop(1, n)
+        def _(d):
+            for t in range(3):
+                col_arrival(t, part, d).wait_recv()
+
+        @pl.loop(part * (share // HD), (part + 1) * (share // HD))
+        def _(h):
+            lanes = pl.ds(pl.multiple_of(h * HD, HD), HD)
+            for start in range(0, cols, width):
+                at = (slice(None), pl.ds(start, width), lanes)
+                got = attend(*(ref[at].reshape(size, HD) for ref in cols_in), allowed)
+                col_out[at] = got.reshape(n, width, HD)
+
+        @pl.loop(1, n)
+        def _(d):
+            back_copy(part, lax.rem(me + d, n)).start()
+
+        @pl.when(stays)
+        def _():
+            rows = pl.ds(pl.multiple_of(slot_here * cols, cols), cols)
+            joined[head, rows, pl.ds(block + part * share, share)] = col_out[
+                me, :, pl.ds(part * share, share)
+            ]
+
+        @pl.when(jnp.logical_not(stays))
+        def _():
+            back_copy(part, me).start()
+
+        if part == 0:
+            onward(PIECES // 2, PIECES)
 
     @pl.loop(0, PIECES)
     def _(s):
@@ -218,52 +262,74 @@
 
     row_copy.wait_recv()
 
-    @pl.loop(0, PIECES)
-    def _(s):
-        w_copy(w_other, index_of(member_sibling, s), 2, sibling, head).wait_recv()
-        w_copy(w_other, index_of(member_far, s), 3, sibling, head).wait_recv()
-
-    for source_head in range(2):
-
+    def back_wait(source_head):
         @pl.loop(0, n // 2)
         def _(slot):
             mine = (head * (n // 2) + slot == me) & (head == source_head)
 
             @pl.when(jnp.logical_not(mine))
             def _():
-                back_arrival(source_head, slot).wait_recv()
-
-    step = 512
-
-    @pl.loop(0, out_ref.shape[1] // step)
-    def _(c):
-        lanes = pl.ds(pl.multiple_of(c * step, step), step)
-        total = jnp.dot(joined[head], w_own[:, lanes], preferred_element_type=jnp.float32)
-        total += jnp.dot(joined[other], w_other[:, lanes], preferred_element_type=jnp.float32)
+                for part in range(PARTS):
+                    back_arrival(source_head, part, slot).wait_recv()
+
+    back_wait(head)
+
+    def own_col_part(lanes):
+        summed[:, lanes] += jnp.dot(
+            joined[head, :, pl.ds(block, block)],
+            w_own[pl.ds(block, block), lanes],
+            preferred_element_type=jnp.float32,
+        )
+
+    tiles(own_col_part)
+
+    @pl.loop(0, PIECES)
+    def _(s):
+        w_copy(w_other, index_of(member_sibling, s), 2, sibling, head).wait_recv()
+        w_copy(w_other, index_of(member_far, s), 3, sibling, head).wait_recv()
+
+    back_wait(other)
+
+    def other_part(lanes):
+        total = summed[:, lanes] + jnp.dot(
+            joined[other], w_other[:, lanes], preferred_element_type=jnp.float32
+        )
         out_ref[:, lanes] = total.astype(jnp.bfloat16)
 
-    for t in range(3):
-
-        @pl.loop(1, n)
-        def _(d):
-            col_copy(t, d).wait_send()
+    tiles(other_part)
+
+    for part in range(PARTS):
+
+        @pl.loop(1, n)
+        def _(d):
+            for t in range(3):
+                col_copy(t, part, d).wait_send()
 
     @pl.loop(0, PIECES)
     def _(s):
         w_copy(w_hbm, index_of(member, s), 0, me, other).wait_send()
-        w_copy(w_other, index_of(member, s), 1, beside, head).wait_send()
         w_copy(w_other, index_of(member, s), 2, sibling, head).wait_send()
         w_copy(w_other, index_of(member_beside, s), 3, sibling, head).wait_send()
 
+    @pl.loop(0, PIECES - STRAIGHT)
+    def _(s):
+        w_copy(w_other, index_of(member, s), 1, beside, head).wait_send()
+
+    @pl.loop(PIECES - STRAIGHT, PIECES)
+    def _(s):
+        w_copy(w_hbm, index_of(member_beside, s), 0, me, other).wait_send()
+
     row_copy.wait_send()
 
-    @pl.loop(1, n)
-    def _(d):
-        back_copy(lax.rem(me + d, n)).wait_send()
-
-    @pl.when(jnp.logical_not(stays))
-    def _():
-        back_copy(me).wait_send()
+    for part in range(PARTS):
+
+        @pl.loop(1, n)
+        def _(d):
+            back_copy(part, lax.rem(me + d, n)).wait_send()
+
+        @pl.when(jnp.logical_not(stays))
+        def _():
+            back_copy(part, me).wait_send()
 
 
 def on_device(n, queries, keys, values, w_out):
@@ -285,13 +351,14 @@
         + [
             pltpu.VMEM((stride, block), bf16),
             pltpu.VMEM((2, half, local_feat), bf16),
+            pltpu.VMEM((half, model_width), jnp.float32),
             pltpu.VMEM((depth, model_width), bf16),
             pltpu.VMEM((depth, model_width), bf16),
             dma((7,)),
-            dma((3, n)),
-            dma((3, n)),
-            dma((n,)),
-            dma((2, n // 2)),
+            dma((3 * PARTS, n)),
+            dma((3 * PARTS, n)),
+            dma((PARTS, n)),
+            dma((2 * PARTS, n // 2)),
             dma((4, 4 * PIECES)),
             dma((4 * PIECES,)),
             dma,

time: 127 us -> 121 us (0.953); the launches traced: 127 us -> 119 us
  Pallas kernels: 122 us -> 114 us
    pallas_call x1, Pallas kernels: 122 us -> 114 us  [on_device(): pl.pallas_call(functools.partial(body, n), out_shape=jax.ShapeDtypeStruct...]
where the time goes in v2:
time: 121 us; the launch traced here: 119 us
  Pallas kernels  114 us (94%)
  local copies, waits for them, and re-layouts  4.7 us (4%)
    pallas_call x1, Pallas kernels, on_device(): pl.pallas_call(functools.partial(body, n), out_shape=jax.ShapeDtypeStruct...  114 us
    unnamed x1, local copies, waits for them, and re-layouts  4.7 us

profile of v2, /device:TPU:29, one launch (start us, length us, event | category | flops | bytes accessed | tf_op | source)
XLA Modules:
  0.0 119.0 jit_solution(2681369314071166058)
XLA Ops:
  0.0 114.3 %shard_map.46 = bf16[512,4096]{1,0:T(8,128)(2,1)} custom-call(bf16[1,1024,1024]{2,1,0:T(8,128)(2,1)} %q_hbm.1, bf16[1,1024,1024]{2,1,0:T(8,128)(2,1)} %k_hbm.1, bf16[1,1024,1024]{2,1,0:T(8,128)(2,1)} %v_hbm.1, bf16[1024,4096]{1,0:T(8,128)(2,1)} %w_hbm.1), custom_call_target="tpu_custom_call" | custom-call | tf_op jit(solution)/shard_map/pallas_call | solution.py:344
  114.3 4.7 %copy.6 = bf16[1,512,4096]{2,1,0:T(8,128)(2,1)} copy(bf16[1,512,4096]{2,1,0:T(8,128)(2,1)} %bitcast.1) | data formatting | bytes 8388608
